TPU v7x, 32 devices: a whole 2x2x4 slice. The times are simulated.
32 devices in a mesh: ba: 8 (over y, x, core), wa: 4 (over z).
Axes of the slice: x: 2, y: 2, z: 4, core: 2. Of those that a mesh axis runs over, the one named last changes fastest.
Arguments:
- sky_model: float32 [2, 2048, 2048], P(None, None, 'wa'), may hold values from -6 to 6
- plane_w: float32 [8], P('ba'), may hold values from -60 to 60
- kernel: float32 [16, 8], replicated, may hold values from -2 to 2
- tile_ids: int32 [512], P(('ba', 'wa')), may hold values from 0 to 255, as said below
- plane_ids: int32 [512, 1], P(('ba', 'wa')), may hold values from 0 to 7; in each aligned block of 16 rows (0 to 15, 16 to 31, ...) at most 2 rows name the same one
- positions: int32 [512, 2, 512], P(('ba', 'wa')), may hold values from 0 to 1935
- observed: float32 [512, 2, 512], P(('ba', 'wa')), may hold values from -6 to 6
Outputs:
- residual_vis: float32 [512, 2, 512], P(('ba', 'wa'))
Inputs may be any that keep to these rules, and one draw needn't show every extreme that they name: `plane_ids`: among the 16 blocks of one device at most 2 name the same w-plane, and in every draw some device has a w-plane named by exactly 2 of its blocks. `tile_ids`: A tile id is row_tile * 16 + column_tile; the blocks held at index a of wa name column tiles a * 4 to (a + 1) * 4 - 1.
All inputs are finite; a program needn't handle non-finite values.
Results may differ from a plain program's by a relative error of at most 0.0003.
Values sent between devices are 32-bit elements; how exact they have to be, the bound alone decides.
A program may use at most 128 MiB of HBM per device.

v0:
```python
import functools
import math

import jax
import jax.numpy as jnp
import numpy as np
from jax import lax
from jax.experimental import pallas as pl
from jax.experimental.pallas import tpu as pltpu
from jax.sharding import PartitionSpec as P

TILE = 128
FIELD_WIDTH = 0.7


def halves(values):
    head = values.astype(jnp.bfloat16)
    rest = (values - head.astype(jnp.float32)).astype(jnp.bfloat16)
    return head, rest


def host_halves(values):
    values = values.astype(np.float32)
    head = values.astype(jnp.bfloat16)
    rest = (values - head.astype(np.float32)).astype(jnp.bfloat16)
    return head, rest


def roots(index, modulus):
    angle = -2.0 * np.pi * (index % modulus) / modulus
    return np.cos(angle), np.sin(angle)


def y_tables(extent):
    panels = extent // TILE
    residue = np.arange(panels, dtype=np.int64)[:, None, None]
    step = np.arange(TILE, dtype=np.int64)[None, :, None]
    row = np.arange(TILE, dtype=np.int64)[None, None, :]
    real, imag = roots((panels * step + residue) * row, extent)
    table = np.concatenate(
        [np.concatenate([real, -imag], axis=2), np.concatenate([imag, real], axis=2)], axis=1
    )
    return host_halves(table)


def x_tables(extent, columns):
    tiles = np.arange(extent // TILE, dtype=np.int64)[:, None, None]
    column = np.arange(columns, dtype=np.int64)[None, :, None]
    cell = np.arange(TILE, dtype=np.int64)[None, None, :]
    real, imag = roots((tiles * TILE + cell) * column, extent)
    return host_halves(np.concatenate([real, imag], axis=2))


def fit(function, top, terms):
    nodes = (np.cos((np.arange(400) + 0.5) * np.pi / 400) + 1.0) * 0.5 * top
    series = np.polynomial.chebyshev.Chebyshev.fit(nodes, function(nodes), terms - 1, domain=[0, top])
    return [float(c) for c in series.convert(kind=np.polynomial.Polynomial).coef]


def horner(coefficients, argument):
    total = coefficients[-1]
    for coefficient in coefficients[-2::-1]:
        total = total * argument + coefficient
    return total


def small_dft(values):
    count = len(values)
    if count == 1:
        return values
    even = small_dft(values[0::2])
    odd = small_dft(values[1::2])
    low, high = [], []
    for k in range(count // 2):
        real, imag = odd[k]
        if k == 0:
            pass
        elif 4 * k == count:
            real, imag = imag, -real
        elif 8 * k == count:
            h = math.sqrt(0.5)
            real, imag = (real + imag) * h, (imag - real) * h
        elif 8 * k == 3 * count:
            h = math.sqrt(0.5)
            real, imag = (imag - real) * h, (real + imag) * -h
        else:
            c = math.cos(-2.0 * math.pi * k / count)
            s = math.sin(-2.0 * math.pi * k / count)
            real, imag = real * c - imag * s, real * s + imag * c
        low.append((even[k][0] + real, even[k][1] + imag))
        high.append((even[k][0] - real, even[k][1] - imag))
    return low + high


def lane_lookup(table, index):
    numbers = lax.GatherDimensionNumbers(
        offset_dims=(),
        collapsed_slice_dims=(1,),
        start_index_map=(1,),
        operand_batching_dims=(0,),
        start_indices_batching_dims=(0,),
    )
    return lax.gather(
        table, index[..., None], numbers, (1, 1), mode=lax.GatherScatterMode.PROMISE_IN_BOUNDS
    )


def dot_exact(head_a, rest_a, head_b, rest_b):
    return jnp.dot(
        jnp.concatenate([head_a, head_a, rest_a], axis=1),
        jnp.concatenate([head_b, rest_b, head_b], axis=0),
        preferred_element_type=jnp.float32,
    )


def y_transform(extent, first, w, sky_ref, work):
    panels = extent // TILE
    lanes = sky_ref.shape[2]
    spacing = FIELD_WIDTH / extent
    edge = 2.0 * (FIELD_WIDTH / 2) ** 2
    lower = fit(lambda r: 1.0 / (1.0 + np.sqrt(1.0 - r)), edge, 7)
    sine = fit(lambda z: np.sin(2 * np.pi * np.sqrt(z)) / np.sqrt(z), 0.25, 7)
    cosine = fit(lambda z: np.cos(2 * np.pi * np.sqrt(z)), 0.25, 7)

    for lane in range(0, lanes, 128):
        x = lax.broadcasted_iota(jnp.int32, (8, 128), 1) + (first + lane)
        x = (x.astype(jnp.float32) - extent / 2) * spacing
        x_sq = x * x

        @pl.loop(0, TILE // 8)
        def _(group):
            base = pl.multiple_of(group * 8, 8)
            row = (lax.broadcasted_iota(jnp.int32, (8, 128), 0) + base).astype(jnp.float32)
            values = []
            for panel in range(panels):
                y = (row + (panel * TILE - extent / 2)) * spacing
                radius = x_sq + y * y
                turns = radius * horner(lower, radius) * w
                turns = turns - jnp.round(turns)
                square = turns * turns
                s = turns * horner(sine, square)
                c = horner(cosine, square)
                real = sky_ref[0, pl.ds(base + panel * TILE, 8), pl.ds(lane, 128)]
                imag = sky_ref[1, pl.ds(base + panel * TILE, 8), pl.ds(lane, 128)]
                values.append((real * c - imag * s, real * s + imag * c))
            for residue, (real, imag) in enumerate(small_dft(values)):
                work[residue, pl.ds(base, 8), pl.ds(lane, 128)] = real
                work[residue, pl.ds(base + TILE, 8), pl.ds(lane, 128)] = imag


def y_finish(extent, start, work, table_head, table_rest, h_head, h_rest):
    panels = extent // TILE
    lanes = work.shape[2]
    per_tile = TILE // panels
    share = 8 // per_tile
    together = 16 // per_tile

    @pl.loop(0, panels // together)
    def _(step):
        products = []
        for i in range(together):
            residue = together * step + i
            head, rest = halves(work[residue])
            products.append(dot_exact(table_head[residue], table_rest[residue], head, rest))
        for part in range(2):
            rows = slice(part * TILE, (part + 1) * TILE)
            grouped = [product[rows].reshape(TILE // 8, 8, lanes) for product in products]
            at = pl.multiple_of(part * TILE + step * 16, 16)
            for place in range(share):
                cut = slice(place * per_tile, (place + 1) * per_tile)
                head, rest = halves(jnp.concatenate([group[:, cut] for group in grouped], axis=1))
                h_head[:, place, pl.ds(at, 16), pl.ds(start, lanes)] = head
                h_rest[:, place, pl.ds(at, 16), pl.ds(start, lanes)] = rest


def plane_kernel(
    extent, slabs, over, unroll,
    tiles_ref, w_ref, sky_ref, asked_ref, taps_ref, y_head, y_rest, e_head, e_rest, out_ref,
    work, h_head, h_rest, yh, yr, eh, er, rows_head, rows_rest, sems,
):
    tiles_across = extent // TILE
    columns = eh.shape[1]
    lanes = sky_ref.shape[2]
    chunk = pl.program_id(0)
    slab = lax.axis_index("wa")
    share = h_head.shape[1]
    copies = [
        pltpu.make_async_copy(source, target, sems.at[i])
        for i, (source, target) in enumerate(((y_head, yh), (y_rest, yr), (e_head, eh), (e_rest, er)))
    ]

    @pl.when(chunk == 0)
    def _():
        for copy in copies:
            copy.start()

    y_transform(extent, slab * columns + chunk * lanes, w_ref[0], sky_ref, work)

    @pl.when(chunk == 0)
    def _():
        copies[0].wait()
        copies[1].wait()

    y_finish(extent, pl.multiple_of(chunk * lanes, lanes), work, yh, yr, h_head, h_rest)

    @pl.when(chunk == columns // lanes - 1)
    def _():
        copies[2].wait()
        copies[3].wait()
        owners, capacity, length = out_ref.shape
        samples = length // 2
        cell = lax.broadcasted_iota(jnp.int32, (1, TILE), 1)
        angle = ((cell * slab) % slabs).astype(jnp.float32) * (-2.0 * math.pi / slabs)
        turn_real = jnp.cos(angle) * (1.0 / extent)
        turn_imag = jnp.sin(angle) * (1.0 / extent)
        per = TILE // tiles_across

        def weights(axis, position):
            place = lax.broadcasted_iota(jnp.int32, (TILE, 128), 0)
            if axis == 1:
                place = (place % per) * tiles_across + place // per
            index = place * over + (over - 1) - position
            table = jnp.broadcast_to(taps_ref[...], (TILE, 128))
            return jnp.where((index & -128) == 0, lane_lookup(table, index & 127), 0.0)

        def form_tile(tile):
            row_tile = tile // tiles_across
            col_tile = tile % tiles_across
            group, place = col_tile // share, col_tile % share
            both = dot_exact(h_head[group, place], h_rest[group, place], eh[row_tile], er[row_tile])
            real = both[:TILE, :TILE] - both[TILE:, TILE:]
            imag = both[:TILE, TILE:] + both[TILE:, :TILE]
            return halves(
                jnp.concatenate(
                    [real * turn_real - imag * turn_imag, real * turn_imag + imag * turn_real], axis=0
                )
            )

        def row_weights(spot, owner, place):
            for lane in range(0, samples, 128):
                head, rest = halves(weights(0, asked_ref[owner, place : place + 1, lane : lane + 128]))
                rows_head[spot, :, lane : lane + 128] = head
                rows_rest[spot, :, lane : lane + 128] = rest

        def predict(spot, owner, place, tile_pair):
            part = dot_exact(*tile_pair, rows_head[spot], rows_rest[spot])
            for lane in range(0, samples, 128):
                at = samples + lane
                column = weights(1, asked_ref[owner, place : place + 1, at : at + 128])
                for c in range(2):
                    values = part[c * TILE : (c + 1) * TILE, lane : lane + 128] * column
                    at = c * samples + lane
                    out_ref[owner, place : place + 1, at : at + 128] = jnp.sum(
                        values, axis=0, keepdims=True
                    )

        @pl.loop(0, owners // unroll)
        def _(step):
            work_list = [(step * unroll + o, c) for o in range(unroll) for c in range(capacity)]
            tiles = [tiles_ref[owner * capacity + c] for owner, c in work_list]
            pairs = {}
            for spot, (owner, c) in enumerate(work_list):
                row_weights(spot, owner, c)
                pairs[spot] = form_tile(tiles[spot])
                if spot:
                    predict(spot - 1, *work_list[spot - 1], pairs.pop(spot - 1))
            predict(spot, *work_list[spot], pairs.pop(spot))


def pack_kernel(planes_ref, tiles_ref, pos_ref, out_ref, used):
    planes, slabs, capacity, length = out_ref.shape
    blocks, _, samples = pos_ref.shape
    for p in range(planes):
        used[p] = 0

    @pl.loop(0, planes)
    def _(p):
        for a in range(slabs):
            out_ref[p, a] = jnp.zeros((capacity, length), jnp.int32)

    @pl.loop(0, blocks)
    def _(b):
        p = planes_ref[b]
        k = used[p]
        used[p] = k + 1
        for place in range(capacity):

            @pl.when(k == place)
            def _():
                for a in range(slabs):
                    for axis in range(2):
                        cut = slice(axis * samples, (axis + 1) * samples)
                        out_ref[p, a, place : place + 1, cut] = pos_ref[b, axis : axis + 1, :]
                    out_ref[p, a, place : place + 1, 2 * samples :] = jnp.full(
                        (1, 128), tiles_ref[b], jnp.int32
                    )


def residual_kernel(planes, slabs, planes_ref, answers_ref, observed_ref, out_ref, used):
    blocks, _, samples = observed_ref.shape
    for p in range(planes):
        used[p] = 0

    @pl.loop(0, blocks)
    def _(b):
        p = planes_ref[b]
        k = used[p]
        used[p] = k + 1
        total = answers_ref[p * slabs]
        for a in range(1, slabs):
            total += answers_ref[p * slabs + a]
        own = total[0:1]
        for place in range(1, total.shape[0]):
            own = jnp.where(k == place, total[place : place + 1], own)
        for c in range(2):
            out_ref[b, c : c + 1, :] = (
                observed_ref[b, c : c + 1, :] - own[:, c * samples : (c + 1) * samples]
            )


def shards(sky_model, plane_w, kernel, tile_ids, plane_ids, positions, observed):
    extent, columns = sky_model.shape[1:]
    planes, slabs = lax.axis_size("ba"), lax.axis_size("wa")
    devices = planes * slabs
    block_count, _, samples = positions.shape
    tiles_across = extent // TILE
    capacity = max(2, block_count // planes)
    target = plane_ids[:, 0]
    axes = ("ba", "wa")
    smem = pl.BlockSpec(memory_space=pltpu.SMEM)
    vmem = pl.BlockSpec(memory_space=pltpu.VMEM)
    hbm = pl.BlockSpec(memory_space=pl.ANY)
    length = 2 * samples + 128

    asked = pl.pallas_call(
        pack_kernel,
        in_specs=[smem, smem, vmem],
        out_specs=vmem,
        out_shape=jax.ShapeDtypeStruct((planes, slabs, capacity, length), jnp.int32),
        scratch_shapes=[pltpu.SMEM((planes,), jnp.int32)],
        name="pack",
    )(target, tile_ids, positions)
    asked = asked.reshape(devices, capacity, length)
    asked = lax.all_to_all(asked, axes, split_axis=0, concat_axis=0, tiled=True)
    asked_tiles = asked[:, :, 2 * samples].reshape(devices * capacity)

    lanes = min(columns, 256)
    share = tiles_across * 8 // TILE
    unroll = math.gcd(devices, 4)
    over, support = kernel.shape
    taps = kernel[::-1, :].T.reshape(1, over * support)
    y_head, y_rest = y_tables(extent)
    e_head, e_rest = x_tables(extent, columns)
    once = pl.Buffered(1)
    answer_shape = (devices, capacity, 2 * samples)
    half = jnp.bfloat16
    values = pl.pallas_call(
        functools.partial(plane_kernel, extent, slabs, over, unroll),
        grid=(columns // lanes,),
        in_specs=[
            smem,
            smem,
            pl.BlockSpec((2, extent, lanes), lambda i: (0, 0, i)),
            pl.BlockSpec(asked.shape, lambda i: (0, 0, 0), pipeline_mode=once),
            pl.BlockSpec(taps.shape, lambda i: (0, 0), pipeline_mode=once),
            hbm, hbm, hbm, hbm,
        ],
        out_specs=pl.BlockSpec(answer_shape, lambda i: (0, 0, 0)),
        out_shape=jax.ShapeDtypeStruct(answer_shape, jnp.float32),
        scratch_shapes=[
            pltpu.VMEM((tiles_across, 2 * TILE, lanes), jnp.float32),
            pltpu.VMEM((tiles_across // share, share, 2 * TILE, columns), half),
            pltpu.VMEM((tiles_across // share, share, 2 * TILE, columns), half),
            pltpu.VMEM(y_head.shape, half),
            pltpu.VMEM(y_head.shape, half),
            pltpu.VMEM(e_head.shape, half),
            pltpu.VMEM(e_head.shape, half),
            pltpu.VMEM((unroll * capacity, TILE, samples), half),
            pltpu.VMEM((unroll * capacity, TILE, samples), half),
            pltpu.SemaphoreType.DMA((4,)),
        ],
        compiler_params=pltpu.CompilerParams(vmem_limit_bytes=60 << 20),
        name="plane",
    )(
        asked_tiles, plane_w, sky_model, asked, taps,
        jnp.asarray(y_head), jnp.asarray(y_rest), jnp.asarray(e_head), jnp.asarray(e_rest),
    )

    answers = lax.all_to_all(values, axes, split_axis=0, concat_axis=0, tiled=True)
    return pl.pallas_call(
        functools.partial(residual_kernel, planes, slabs),
        in_specs=[smem, vmem, vmem],
        out_specs=vmem,
        out_shape=jax.ShapeDtypeStruct(observed.shape, jnp.float32),
        scratch_shapes=[pltpu.SMEM((planes,), jnp.int32)],
        name="residual",
    )(target, answers, observed)


def solution(mesh):
    return jax.shard_map(
        shards,
        mesh=mesh,
        in_specs=(
            P(None, None, "wa"),
            P("ba"),
            P(),
            P(("ba", "wa")),
            P(("ba", "wa"), None),
            P(("ba", "wa"), None, None),
            P(("ba", "wa"), None, None),
        ),
        out_specs=P(("ba", "wa"), None, None),
        check_vma=False,
    )
```

profile of v0, /device:TPU:0, one launch (start us, length us, event | category | flops | bytes accessed | tf_op | source)
XLA Modules:
  0.0 82.7 jit_solution(5068139013003997137)
XLA Ops:
  0.0 2.0 %pack.1 = s32[8,4,2,1152]{3,2,1,0:T(2,128)} custom-call(s32[16]{0:T(128)} %bitcast.5, s32[16]{0:T(128)} %tiles_ref.1, s32[16,2,512]{2,1,0:T(2,128)} %pos_ref.1), custom_call_target="tpu_custom_call" | custom-call | tf_op jit(solution)/shard_map/pack/pallas_call | solution.py:335
  2.0 7.3 %all-to-all-start = ((s32[32,2,1152]{2,1,0:T(2,128)}), s32[32,2,1152]{2,1,0:T(2,128)S(1)}, u32[]{:S(2)}, u32[]{:S(2)}) async-start(s32[32,2,1152]{2,1,0:T(2,128)} %bitcast.3), calls=%async_computation | async-start | bytes 589824 | tf_op jit(solution)/shard_map/all_to_all | solution.py:344
  9.3 0.8 rev.3
  10.1 0.6 reshape.7.taps_ref
  11.4 8.7 %all-to-all-done.asked_ref = s32[32,2,1152]{2,1,0:T(2,128)S(1)} async-done(((s32[32,2,1152]{2,1,0:T(2,128)}), s32[32,2,1152]{2,1,0:T(2,128)S(1)}, u32[]{:S(2)}, u32[]{:S(2)}) %all-to-all-start) | async-done | bytes 294944 | tf_op jit(solution)/shard_map/all_to_all | solution.py:344
  20.0 0.0 copy-start
  20.0 0.6 slice_reduce_fusion
  20.7 0.6 reshape_squeeze.3.tiles_ref
  21.3 0.0 copy-done
  21.3 46.1 %plane.1 = f32[32,2,1024]{2,1,0:T(2,128)} custom-call(s32[64]{0:T(128)} %reshape_squeeze.3.tiles_ref, f32[1]{0:T(128)S(6)} %copy.12.w_ref, f32[2,2048,512]{2,1,0:T(8,128)} %sky_ref.1, s32[32,2,1152]{2,1,0:T(2,128)} %copy-done, f32[1,128]{1,0:T(1,128)} %reshape.7.taps_ref, bf16[16,256,256]{2,1,0:T(8,128)(2,1)} %constant.8.clone.y_head, ...), custom_call_target="tpu_custom_call" | custom-call | tf_op jit(solution)/shard_map/plane/pallas_call | solution.py:357
  67.4 13.5 %all_to_all.10.answers_ref = f32[32,2,1024]{2,1,0:T(2,128)} all-to-all(f32[32,2,1024]{2,1,0:T(2,128)} %plane.1), channel_id=1, replica_groups=mesh['ba'=8,'wa'=4] {'ba','wa'}, dimensions={0} | all-to-all | bytes 524288 | tf_op jit(solution)/shard_map/all_to_all | solution.py:389
  80.9 1.8 %residual.1 = f32[16,2,512]{2,1,0:T(2,128)} custom-call(s32[16]{0:T(128)} %bitcast.6, f32[32,2,1024]{2,1,0:T(2,128)} %all_to_all.10.answers_ref, f32[16,2,512]{2,1,0:T(2,128)} %observed_ref.1), custom_call_target="tpu_custom_call" | custom-call | tf_op jit(solution)/shard_map/residual/pallas_call | solution.py:390
Async XLA Ops:
  2.0 18.0 %all-to-all-start = ((s32[32,2,1152]{2,1,0:T(2,128)}), s32[32,2,1152]{2,1,0:T(2,128)S(1)}, u32[]{:S(2)}, u32[]{:S(2)}) async-start(s32[32,2,1152]{2,1,0:T(2,128)} %bitcast.3), calls=%async_computation | async-start | bytes 589824 | tf_op jit(solution)/shard_map/all_to_all | solution.py:344
  20.0 1.2 %copy-start = (s32[32,2,1152]{2,1,0:T(2,128)}, s32[32,2,1152]{2,1,0:T(2,128)S(1)}, u32[]{:S(2)}) copy-start(s32[32,2,1152]{2,1,0:T(2,128)S(1)} %all-to-all-done.asked_ref) | copy-start | bytes 884740
where the time goes:
time: 83.1 us; the launch traced here: 82.7 us
  Pallas kernels  49.9 us (60%)
  blocking collectives  13.5 us (16%)
  waiting for transfers between devices  8.66 us (10%)
  starting transfers between devices  7.33 us (9%)
  local copies, waits for them, and re-layouts  2.62 us (3%)
    pallas_call x1, Pallas kernels, shards(): pl.pallas_call(functools.partial(plane_kernel, extent, slabs, over, unrol...  46.1 us
    all_to_all x1, blocking collectives, shards(): lax.all_to_all(values, axes, split_axis=0, concat_axis=0, tiled=True)  13.5 us
    all_to_all x1, waiting for transfers between devices, shards(): asked = lax.all_to_all(asked, axes, split_axis=0, concat_axis=0, tiled=True)  8.66 us
    all_to_all x1, starting transfers between devices, shards(): asked = lax.all_to_all(asked, axes, split_axis=0, concat_axis=0, tiled=True)  7.33 us
    pallas_call x1, Pallas kernels, shards(): pl.pallas_call(pack_kernel, in_specs=[smem, smem, vmem], out_specs=vmem,...  2.01 us
    pallas_call x1, Pallas kernels, shards(): pl.pallas_call(functools.partial(residual_kernel, planes, slabs), in_spec...  1.82 us
  transfers between devices with their start and end apart: 1, of which 1 were waited for; matrix products, arithmetic and copies ran while one was open for 2% of the time, Pallas kernels for 0%

commit v1 on v0

v1 whole, which is shorter than its diff:
```python
import functools
import math

import jax
import jax.numpy as jnp
import numpy as np
from jax import lax
from jax.experimental import pallas as pl
from jax.experimental.pallas import tpu as pltpu
from jax.sharding import PartitionSpec as P

TILE = 128
FIELD_WIDTH = 0.7


def halves(values):
    head = values.astype(jnp.bfloat16)
    rest = (values - head.astype(jnp.float32)).astype(jnp.bfloat16)
    return head, rest


def host_halves(values):
    values = values.astype(np.float32)
    head = values.astype(jnp.bfloat16)
    rest = (values - head.astype(np.float32)).astype(jnp.bfloat16)
    return head, rest


def roots(index, modulus):
    angle = -2.0 * np.pi * (index % modulus) / modulus
    return np.cos(angle), np.sin(angle)


def y_tables(extent):
    panels = extent // TILE
    residue = np.arange(panels, dtype=np.int64)[:, None, None]
    step = np.arange(TILE, dtype=np.int64)[None, :, None]
    row = np.arange(TILE, dtype=np.int64)[None, None, :]
    real, imag = roots((panels * step + residue) * row, extent)
    table = np.concatenate(
        [np.concatenate([real, -imag], axis=2), np.concatenate([imag, real], axis=2)], axis=1
    )
    return host_halves(table)


def x_tables(extent, columns):
    tiles = np.arange(extent // TILE, dtype=np.int64)[:, None, None]
    column = np.arange(columns, dtype=np.int64)[None, :, None]
    cell = np.arange(TILE, dtype=np.int64)[None, None, :]
    real, imag = roots((tiles * TILE + cell) * column, extent)
    return host_halves(np.concatenate([real, imag], axis=2))


def fit(function, top, terms):
    nodes = (np.cos((np.arange(400) + 0.5) * np.pi / 400) + 1.0) * 0.5 * top
    series = np.polynomial.chebyshev.Chebyshev.fit(nodes, function(nodes), terms - 1, domain=[0, top])
    return [float(c) for c in series.convert(kind=np.polynomial.Polynomial).coef]


def horner(coefficients, argument):
    total = coefficients[-1]
    for coefficient in coefficients[-2::-1]:
        total = total * argument + coefficient
    return total


def small_dft(values):
    count = len(values)
    if count == 1:
        return values
    even = small_dft(values[0::2])
    odd = small_dft(values[1::2])
    low, high = [], []
    for k in range(count // 2):
        real, imag = odd[k]
        if k == 0:
            pass
        elif 4 * k == count:
            real, imag = imag, -real
        elif 8 * k == count:
            h = math.sqrt(0.5)
            real, imag = (real + imag) * h, (imag - real) * h
        elif 8 * k == 3 * count:
            h = math.sqrt(0.5)
            real, imag = (imag - real) * h, (real + imag) * -h
        else:
            c = math.cos(-2.0 * math.pi * k / count)
            s = math.sin(-2.0 * math.pi * k / count)
            real, imag = real * c - imag * s, real * s + imag * c
        low.append((even[k][0] + real, even[k][1] + imag))
        high.append((even[k][0] - real, even[k][1] - imag))
    return low + high


def lane_lookup(table, index):
    numbers = lax.GatherDimensionNumbers(
        offset_dims=(),
        collapsed_slice_dims=(1,),
        start_index_map=(1,),
        operand_batching_dims=(0,),
        start_indices_batching_dims=(0,),
    )
    return lax.gather(
        table, index[..., None], numbers, (1, 1), mode=lax.GatherScatterMode.PROMISE_IN_BOUNDS
    )


def dot_exact(head_a, rest_a, head_b, rest_b):
    return jnp.dot(
        jnp.concatenate([head_a, head_a, rest_a], axis=1),
        jnp.concatenate([head_b, rest_b, head_b], axis=0),
        preferred_element_type=jnp.float32,
    )


def y_transform(extent, first, start, lanes, w, sky_ref, work):
    panels = extent // TILE
    spacing = FIELD_WIDTH / extent
    edge = 2.0 * (FIELD_WIDTH / 2) ** 2
    lower = fit(lambda r: 1.0 / (1.0 + np.sqrt(1.0 - r)), edge, 7)
    sine = fit(lambda z: np.sin(2 * np.pi * np.sqrt(z)) / np.sqrt(z), 0.25, 7)
    cosine = fit(lambda z: np.cos(2 * np.pi * np.sqrt(z)), 0.25, 7)

    for lane in range(0, lanes, 128):
        x = lax.broadcasted_iota(jnp.int32, (8, 128), 1) + (first + lane)
        x = (x.astype(jnp.float32) - extent / 2) * spacing
        x_sq = x * x

        @pl.loop(0, TILE // 8)
        def _(group):
            base = pl.multiple_of(group * 8, 8)
            row = (lax.broadcasted_iota(jnp.int32, (8, 128), 0) + base).astype(jnp.float32)
            values = []
            for panel in range(panels):
                y = (row + (panel * TILE - extent / 2)) * spacing
                radius = x_sq + y * y
                turns = radius * horner(lower, radius) * w
                turns = turns - jnp.round(turns)
                square = turns * turns
                s = turns * horner(sine, square)
                c = horner(cosine, square)
                real = sky_ref[0, pl.ds(base + panel * TILE, 8), pl.ds(start + lane, 128)]
                imag = sky_ref[1, pl.ds(base + panel * TILE, 8), pl.ds(start + lane, 128)]
                values.append((real * c - imag * s, real * s + imag * c))
            for residue, (real, imag) in enumerate(small_dft(values)):
                work[residue, pl.ds(base, 8), pl.ds(lane, 128)] = real
                work[residue, pl.ds(base + TILE, 8), pl.ds(lane, 128)] = imag


def y_finish(extent, start, work, table_head, table_rest, h_head, h_rest):
    panels = extent // TILE
    lanes = work.shape[2]
    per_tile = TILE // panels
    share = 8 // per_tile
    together = 16 // per_tile

    @pl.loop(0, panels // together)
    def _(step):
        products = []
        for i in range(together):
            residue = together * step + i
            head, rest = halves(work[residue])
            products.append(dot_exact(table_head[residue], table_rest[residue], head, rest))
        for part in range(2):
            rows = slice(part * TILE, (part + 1) * TILE)
            grouped = [product[rows].reshape(TILE // 8, 8, lanes) for product in products]
            at = pl.multiple_of(part * TILE + step * 16, 16)
            for place in range(share):
                cut = slice(place * per_tile, (place + 1) * per_tile)
                head, rest = halves(jnp.concatenate([group[:, cut] for group in grouped], axis=1))
                h_head[:, place, pl.ds(at, 16), pl.ds(start, lanes)] = head
                h_rest[:, place, pl.ds(at, 16), pl.ds(start, lanes)] = rest


def build_taps(taps_ref):
    over, support = taps_ref.shape
    lane = lax.broadcasted_iota(jnp.int32, (1, over * support), 1)
    table = jnp.zeros((1, over * support), jnp.float32)
    for o in range(over):
        for k in range(support):
            table = jnp.where(lane == k * over + (over - 1 - o), taps_ref[o, k], table)
    return table


def plane_kernel(
    extent, lanes, unroll,
    planes_ref, tiles_ref, w_ref, kernel_ref, pos_ref, sky_hbm, y_head, y_rest, e_head, e_rest,
    out_ref,
    sky, work, h_head, h_rest, yh, yr, eh, er, rows_head, rows_rest,
    send, asked, asked_tiles, values, answers, taps,
    local_sems, request_send, request_recv, answer_send, answer_recv, tile_sem,
):
    tiles_across = extent // TILE
    columns = eh.shape[1]
    share = h_head.shape[1]
    planes, slabs = lax.axis_size("ba"), lax.axis_size("wa")
    devices = planes * slabs
    plane, slab = lax.axis_index("ba"), lax.axis_index("wa")
    me = plane * slabs + slab
    blocks, _, samples = pos_ref.shape
    capacity = send.shape[1]
    over = kernel_ref.shape[0]

    chunks = columns // lanes
    loads = [
        pltpu.make_async_copy(
            sky_hbm.at[:, :, pl.ds(i * lanes, lanes)], sky.at[:, :, pl.ds(i * lanes, lanes)], local_sems.at[4 + i]
        )
        for i in range(chunks)
    ]
    copies = [
        pltpu.make_async_copy(source, target, local_sems.at[i])
        for i, (source, target) in enumerate(((y_head, yh), (y_rest, yr), (e_head, eh), (e_rest, er)))
    ]
    loads[0].start()
    copies[0].start()
    copies[1].start()
    for load in loads[1:]:
        load.start()
    copies[2].start()
    copies[3].start()

    def peer(offset):
        index = lax.rem(me + offset, devices)
        return index, {"ba": index // slabs, "wa": index % slabs}

    barrier = pltpu.get_barrier_semaphore()

    @pl.loop(1, devices)
    def _(offset):
        pl.semaphore_signal(
            barrier, inc=1, device_id=peer(offset)[1], device_id_type=pl.DeviceIdType.MESH
        )

    @pl.loop(0, planes)
    def _(p):
        count = jnp.int32(0)
        found = [jnp.int32(0)] * capacity
        for b in range(blocks):
            match = planes_ref[b, 0] == p
            for c in range(capacity):
                found[c] = jnp.where(match & (count == c), b, found[c])
            count = count + jnp.where(match, 1, 0)
        for c in range(capacity):
            b = found[c]
            for axis in range(2):
                send[p, c : c + 1, axis * samples : (axis + 1) * samples] = pos_ref[b, axis : axis + 1, :]
            send[p, c : c + 1, 2 * samples :] = jnp.full((1, 128), tiles_ref[b], jnp.int32)

    taps[...] = build_taps(kernel_ref)

    pl.semaphore_wait(barrier, devices - 1)

    def request(offset):
        index, where = peer(offset)
        return pltpu.make_async_remote_copy(
            src_ref=send.at[index // slabs],
            dst_ref=asked.at[me],
            send_sem=request_send.at[offset],
            recv_sem=request_recv.at[offset],
            device_id=where,
            device_id_type=pl.DeviceIdType.MESH,
        )

    @pl.loop(1, devices)
    def _(offset):
        request(offset).start()

    asked[me] = send[plane]

    for i in range(chunks):
        loads[i].wait()
        y_transform(extent, slab * columns + i * lanes, i * lanes, lanes, w_ref[0], sky, work)
        if i == 0:
            copies[0].wait()
            copies[1].wait()
        y_finish(extent, i * lanes, work, yh, yr, h_head, h_rest)

    copies[2].wait()
    copies[3].wait()

    @pl.loop(1, devices)
    def _(offset):
        request(offset).wait()

    tile_copy = pltpu.make_async_copy(asked.at[:, :, pl.ds(2 * samples, 128)], asked_tiles, tile_sem)
    tile_copy.start()
    tile_copy.wait()

    cell = lax.broadcasted_iota(jnp.int32, (1, TILE), 1)
    angle = ((cell * slab) % slabs).astype(jnp.float32) * (-2.0 * math.pi / slabs)
    turn_real = jnp.cos(angle) * (1.0 / extent)
    turn_imag = jnp.sin(angle) * (1.0 / extent)
    per = TILE // tiles_across

    def weights(axis, position):
        place = lax.broadcasted_iota(jnp.int32, (TILE, 128), 0)
        if axis == 1:
            place = (place % per) * tiles_across + place // per
        index = place * over + (over - 1) - position
        table = jnp.broadcast_to(taps[...], (TILE, 128))
        return jnp.where((index & -128) == 0, lane_lookup(table, index & 127), 0.0)

    def form_tile(tile):
        row_tile = tile // tiles_across
        col_tile = tile % tiles_across
        group, place = col_tile // share, col_tile % share
        both = dot_exact(h_head[group, place], h_rest[group, place], eh[row_tile], er[row_tile])
        real = both[:TILE, :TILE] - both[TILE:, TILE:]
        imag = both[:TILE, TILE:] + both[TILE:, :TILE]
        return halves(
            jnp.concatenate(
                [real * turn_real - imag * turn_imag, real * turn_imag + imag * turn_real], axis=0
            )
        )

    def row_weights(spot, owner, place):
        for lane in range(0, samples, 128):
            head, rest = halves(weights(0, asked[owner, place : place + 1, lane : lane + 128]))
            rows_head[spot, :, lane : lane + 128] = head
            rows_rest[spot, :, lane : lane + 128] = rest

    def predict(spot, owner, place, tile_pair):
        part = dot_exact(*tile_pair, rows_head[spot], rows_rest[spot])
        for lane in range(0, samples, 128):
            at = samples + lane
            column = weights(1, asked[owner, place : place + 1, at : at + 128])
            for c in range(2):
                outcome = part[c * TILE : (c + 1) * TILE, lane : lane + 128] * column
                at = c * samples + lane
                values[owner, place : place + 1, at : at + 128] = jnp.sum(outcome, axis=0, keepdims=True)

    def answer(offset):
        index, where = peer(offset)
        return pltpu.make_async_remote_copy(
            src_ref=values.at[index],
            dst_ref=answers.at[me],
            send_sem=answer_send.at[offset],
            recv_sem=answer_recv.at[offset],
            device_id=where,
            device_id_type=pl.DeviceIdType.MESH,
        )

    steps = devices // unroll

    @pl.loop(0, steps)
    def _(step):
        @pl.when(step > 0)
        def _():
            for o in range(unroll):
                answer((step - 1) * unroll + o + 1).start()

        work_list = [(peer(step * unroll + o + 1)[0], c) for o in range(unroll) for c in range(capacity)]
        tiles = [asked_tiles[owner, c, 0] for owner, c in work_list]
        pairs = {}
        for spot, (owner, c) in enumerate(work_list):
            row_weights(spot, owner, c)
            pairs[spot] = form_tile(tiles[spot])
            if spot:
                predict(spot - 1, *work_list[spot - 1], pairs.pop(spot - 1))
        predict(spot, *work_list[spot], pairs.pop(spot))

    for o in range(unroll - 1):
        answer((steps - 1) * unroll + o + 1).start()
    answers[me] = values[me]

    @pl.loop(1, devices)
    def _(offset):
        answer(offset).wait()

    @pl.loop(0, blocks)
    def _(b):
        p = planes_ref[b, 0]
        k = jnp.int32(0)
        for earlier in range(blocks):
            k = k + jnp.where((planes_ref[earlier, 0] == p) & (earlier < b), 1, 0)
        total = answers[p * slabs]
        for a in range(1, slabs):
            total += answers[p * slabs + a]
        own = total[0:1]
        for place in range(1, capacity):
            own = jnp.where(k == place, total[place : place + 1], own)
        for c in range(2):
            out_ref[b, c : c + 1, :] = own[:, c * samples : (c + 1) * samples]


def shards(sky_model, plane_w, kernel, tile_ids, plane_ids, positions, observed):
    extent, columns = sky_model.shape[1:]
    planes, slabs = lax.axis_size("ba"), lax.axis_size("wa")
    devices = planes * slabs
    block_count, _, samples = positions.shape
    tiles_across = extent // TILE
    capacity = max(2, block_count // planes)
    smem = pl.BlockSpec(memory_space=pltpu.SMEM)
    vmem = pl.BlockSpec(memory_space=pltpu.VMEM)
    hbm = pl.BlockSpec(memory_space=pl.ANY)
    length = 2 * samples + 128

    lanes = min(columns, 256)
    share = tiles_across * 8 // TILE
    unroll = math.gcd(devices, 4)
    over, support = kernel.shape
    y_head, y_rest = y_tables(extent)
    e_head, e_rest = x_tables(extent, columns)
    half = jnp.bfloat16
    dma = pltpu.SemaphoreType.DMA
    predicted = pl.pallas_call(
        functools.partial(plane_kernel, extent, lanes, unroll),
        in_specs=[smem, smem, smem, smem, vmem, hbm, hbm, hbm, hbm, hbm],
        out_specs=vmem,
        out_shape=jax.ShapeDtypeStruct(observed.shape, jnp.float32),
        scratch_shapes=[
            pltpu.VMEM((2, extent, columns), jnp.float32),
            pltpu.VMEM((tiles_across, 2 * TILE, lanes), jnp.float32),
            pltpu.VMEM((tiles_across // share, share, 2 * TILE, columns), half),
            pltpu.VMEM((tiles_across // share, share, 2 * TILE, columns), half),
            pltpu.VMEM(y_head.shape, half),
            pltpu.VMEM(y_head.shape, half),
            pltpu.VMEM(e_head.shape, half),
            pltpu.VMEM(e_head.shape, half),
            pltpu.VMEM((unroll * capacity, TILE, samples), half),
            pltpu.VMEM((unroll * capacity, TILE, samples), half),
            pltpu.VMEM((planes, capacity, length), jnp.int32),
            pltpu.VMEM((devices, capacity, length), jnp.int32),
            pltpu.SMEM((devices, capacity, 128), jnp.int32),
            pltpu.VMEM((devices, capacity, 2 * samples), jnp.float32),
            pltpu.VMEM((devices, capacity, 2 * samples), jnp.float32),
            pltpu.VMEM((1, over * support), jnp.float32),
            dma((4 + columns // lanes,)),
            dma((devices,)),
            dma((devices,)),
            dma((devices,)),
            dma((devices,)),
            dma,
        ],
        compiler_params=pltpu.CompilerParams(
            vmem_limit_bytes=60 << 20, collective_id=0, has_side_effects=True
        ),
        name="plane",
    )(
        plane_ids, tile_ids, plane_w, kernel, positions, sky_model,
        jnp.asarray(y_head), jnp.asarray(y_rest), jnp.asarray(e_head), jnp.asarray(e_rest),
    )
    return observed - predicted


def solution(mesh):
    return jax.shard_map(
        shards,
        mesh=mesh,
        in_specs=(
            P(None, None, "wa"),
            P("ba"),
            P(),
            P(("ba", "wa")),
            P(("ba", "wa"), None),
            P(("ba", "wa"), None, None),
            P(("ba", "wa"), None, None),
        ),
        out_specs=P(("ba", "wa"), None, None),
        check_vma=False,
    )
```

time: 83.1 us -> 63.2 us (0.76)
  blocking collectives: 13.5 us -> 0 us
  waiting for transfers between devices: 8.66 us -> 0 us
  Pallas kernels: 49.9 us -> 58.1 us
  starting transfers between devices: 7.33 us -> 0 us
  other arithmetic: 0 us -> 1.51 us
    all_to_all x1 -> x0, blocking collectives: 13.5 us -> none  [shards(): lax.all_to_all(values, axes, split_axis=0, concat_axis=0, tiled=True)]
    all_to_all x1 -> x0, waiting for transfers between devices: 8.66 us -> none  [shards(): asked = lax.all_to_all(asked, axes, split_axis=0, concat_axis=0, tiled=True)]
    pallas_call x3 -> x1, Pallas kernels: 49.9 us -> 58.1 us  [shards(): pl.pallas_call(functools.partial(plane_kernel, extent, lanes, unroll), in...]
    all_to_all x1 -> x0, starting transfers between devices: 7.33 us -> none  [shards(): asked = lax.all_to_all(asked, axes, split_axis=0, concat_axis=0, tiled=True)]
    unnamed x2 -> x4, local copies, waits for them, and re-layouts: 0.01 us -> 2.69 us
    sub x0 -> x1, other arithmetic: none -> 1.51 us  [shards(): return observed - predicted]
  transfers between devices with their start and end apart: 1 -> 0, of which waited for: 1 -> 0; matrix products, arithmetic and copies ran while one was open for 2% -> 0% of each run, Pallas kernels for 0% -> 0%
where the time goes in v1:
time: 63.2 us; the launch traced here: 63 us
  Pallas kernels  58.1 us (92%)
  local copies, waits for them, and re-layouts  2.69 us (4%)
  other arithmetic  1.51 us (2%)
  between operations  0.67 us (1%)
    pallas_call x1, Pallas kernels, shards(): pl.pallas_call(functools.partial(plane_kernel, extent, lanes, unroll), in...  58.1 us
    unnamed x4, local copies, waits for them, and re-layouts  2.69 us
    sub x1, other arithmetic, shards(): return observed - predicted  1.51 us

profile of v1, /device:TPU:0, one launch (start us, length us, event | category | flops | bytes accessed | tf_op | source)
XLA Modules:
  0.0 63.0 jit_solution(12061707084963332018)
XLA Ops:
  0.7 1.4 %copy.13.kernel_ref = f32[16,8]{1,0:T(8,128)} copy(f32[16,8]{0,1:T(8,128)} %param.13) | data formatting | bytes 1024 | tf_op args[2]
  2.0 1.3 %copy.12.planes_ref = s32[16,1]{1,0:T(8,128)} copy(s32[16,1]{0,1:T(1,128)} %param.15) | data formatting | bytes 128 | tf_op args[4]
  3.3 0.0 copy-start
  3.3 58.1 %plane.1 = f32[16,2,512]{2,1,0:T(2,128)} custom-call(s32[16,1]{1,0:T(8,128)} %copy.12.planes_ref, s32[16]{0:T(128)} %tiles_ref.1, f32[1]{0:T(128)S(6)} %copy.14.w_ref, f32[16,8]{1,0:T(8,128)} %copy.13.kernel_ref, s32[16,2,512]{2,1,0:T(2,128)} %pos_ref.1, f32[2,2048,512]{2,1,0:T(8,128)} %sky_hbm.1, bf16[16,256,256]{2,1,0:T(8,128)(2,1)} %constant.8.clone.y_head, ...), custom_call_target="tpu_custom_call" | custom-call | tf_op jit(solution)/shard_map/plane/pallas_call | solution.py:407
  61.4 0.0 copy-done
  61.5 1.5 %sub.3 = f32[16,2,512]{2,1,0:T(2,128)} subtract(f32[16,2,512]{2,1,0:T(2,128)S(1)} %copy-done, f32[16,2,512]{2,1,0:T(2,128)} %plane.1) | non-fusion elementwise | flops 16384 | bytes 196608 | tf_op jit(solution)/shard_map/sub | solution.py:444
Async XLA Ops:
  3.3 58.1 %copy-start = (f32[16,2,512]{2,1,0:T(2,128)S(1)}, f32[16,2,512]{2,1,0:T(2,128)}, u32[]{:S(2)}) copy-start(f32[16,2,512]{2,1,0:T(2,128)} %param.17) | copy-start | bytes 196612

commit v2 on v1

v2 whole, which is shorter than its diff:
```python
import functools
import math

import jax
import jax.numpy as jnp
import numpy as np
from jax import lax
from jax.experimental import pallas as pl
from jax.experimental.pallas import tpu as pltpu
from jax.sharding import PartitionSpec as P

TILE = 128
FIELD_WIDTH = 0.7


def halves(values):
    head = values.astype(jnp.bfloat16)
    rest = (values - head.astype(jnp.float32)).astype(jnp.bfloat16)
    return head, rest


def host_halves(values):
    values = values.astype(np.float32)
    head = values.astype(jnp.bfloat16)
    rest = (values - head.astype(np.float32)).astype(jnp.bfloat16)
    return head, rest


def roots(index, modulus):
    angle = -2.0 * np.pi * (index % modulus) / modulus
    return np.cos(angle), np.sin(angle)


def y_tables(extent):
    panels = extent // TILE
    residue = np.arange(panels, dtype=np.int64)[:, None, None]
    step = np.arange(TILE, dtype=np.int64)[None, :, None]
    row = np.arange(TILE, dtype=np.int64)[None, None, :]
    real, imag = roots((panels * step + residue) * row, extent)
    table = np.concatenate(
        [np.concatenate([real, -imag], axis=2), np.concatenate([imag, real], axis=2)], axis=1
    )
    return host_halves(table)


def x_tables(extent, columns):
    tiles = np.arange(extent // TILE, dtype=np.int64)[:, None, None]
    pair = np.arange(columns // 2, dtype=np.int64)[None, :, None]
    cell = np.arange(TILE, dtype=np.int64)[None, None, :]
    real, imag = roots((tiles * TILE + cell) * (2 * pair + 1), 2 * extent)
    return np.concatenate(host_halves(np.concatenate([real, -imag], axis=1)), axis=2)


def fit(function, top, terms):
    nodes = (np.cos((np.arange(400) + 0.5) * np.pi / 400) + 1.0) * 0.5 * top
    series = np.polynomial.chebyshev.Chebyshev.fit(nodes, function(nodes), terms - 1, domain=[0, top])
    return [float(c) for c in series.convert(kind=np.polynomial.Polynomial).coef]


def horner(coefficients, argument):
    total = coefficients[-1]
    for coefficient in coefficients[-2::-1]:
        total = total * argument + coefficient
    return total


def small_dft(values):
    count = len(values)
    if count == 1:
        return values
    even = small_dft(values[0::2])
    odd = small_dft(values[1::2])
    low, high = [], []
    for k in range(count // 2):
        real, imag = odd[k]
        if k == 0:
            pass
        elif 4 * k == count:
            real, imag = imag, -real
        elif 8 * k == count:
            h = math.sqrt(0.5)
            real, imag = (real + imag) * h, (imag - real) * h
        elif 8 * k == 3 * count:
            h = math.sqrt(0.5)
            real, imag = (imag - real) * h, (real + imag) * -h
        else:
            c = math.cos(-2.0 * math.pi * k / count)
            s = math.sin(-2.0 * math.pi * k / count)
            real, imag = real * c - imag * s, real * s + imag * c
        low.append((even[k][0] + real, even[k][1] + imag))
        high.append((even[k][0] - real, even[k][1] - imag))
    return low + high


def lane_lookup(table, index):
    numbers = lax.GatherDimensionNumbers(
        offset_dims=(),
        collapsed_slice_dims=(1,),
        start_index_map=(1,),
        operand_batching_dims=(0,),
        start_indices_batching_dims=(0,),
    )
    return lax.gather(
        table, index[..., None], numbers, (1, 1), mode=lax.GatherScatterMode.PROMISE_IN_BOUNDS
    )


def dot_exact(head_a, rest_a, head_b, rest_b):
    return jnp.dot(
        jnp.concatenate([head_a, head_a, rest_a], axis=1),
        jnp.concatenate([head_b, rest_b, head_b], axis=0),
        preferred_element_type=jnp.float32,
    )


def interpolation(nodes):
    place = (np.arange(nodes) + 0.5) * np.pi / nodes
    at = np.arccos((np.arange(TILE) - (TILE - 1) / 2) / (TILE / 2))
    order = np.arange(nodes)
    scale = np.where(order == 0, 1.0, 2.0) / nodes
    head, rest = host_halves((np.cos(at[:, None] * order) * scale) @ np.cos(order[:, None] * place))
    return np.concatenate([head, head, rest], axis=1)


def y_phases(extent, first, stride, lanes, w, basis_ref, phases):
    panels = extent // TILE
    nodes = basis_ref.shape[1] // 3
    spacing = FIELD_WIDTH / extent
    edge = 2.0 * (FIELD_WIDTH / 2 * (1.0 + TILE / extent)) ** 2
    lower = fit(lambda r: 1.0 / (1.0 + np.sqrt(1.0 - r)), edge, 7)
    sine = fit(lambda z: np.sin(2 * np.pi * np.sqrt(z)) / np.sqrt(z), 0.25, 7)
    cosine = fit(lambda z: np.cos(2 * np.pi * np.sqrt(z)), 0.25, 7)
    x = lax.broadcasted_iota(jnp.int32, (nodes, lanes), 1) * stride + first
    x = (x.astype(jnp.float32) - extent / 2) * spacing
    x_sq = x * x
    node = lax.broadcasted_iota(jnp.int32, (nodes, 128), 0).astype(jnp.float32)
    node = jnp.cos((node + 0.5) * (math.pi / nodes)) * (TILE / 2) + (TILE - 1) / 2
    node = jnp.concatenate([node] * (lanes // 128), axis=1)
    basis = basis_ref[...]
    unroll = math.gcd(panels, 8)

    @pl.loop(0, panels // unroll)
    def _(step):
        for i in range(unroll):
            panel = step * unroll + i
            y = (node + ((panel * TILE).astype(jnp.float32) - extent / 2)) * spacing
            radius = x_sq + y * y
            turns = radius * horner(lower, radius) * w
            turns = turns - jnp.round(turns)
            square = turns * turns
            both = jnp.concatenate([horner(cosine, square), turns * horner(sine, square)], axis=1)
            head, rest = halves(both)
            phases[panel] = jnp.dot(
                basis, jnp.concatenate([head, rest, head], axis=0), preferred_element_type=jnp.float32
            )


def y_combine(extent, side, lanes, sky_ref, phases, work):
    panels = extent // TILE

    @pl.loop(0, TILE // 8)
    def _(group):
        base = pl.multiple_of(group * 8, 8)
        mirror = 127 - lax.broadcasted_iota(jnp.int32, (8, 128), 1)
        for lane in range(0, lanes, 128):
            at = lanes + lane if side else lanes - 128 - lane
            values = []
            for panel in range(panels):
                c = phases[panel, pl.ds(base, 8), pl.ds(lane, 128)]
                s = phases[panel, pl.ds(base, 8), pl.ds(lanes + lane, 128)]
                real, imag = (
                    sky_ref[part, pl.ds(base + panel * TILE, 8), pl.ds(at, 128)] for part in range(2)
                )
                if not side:
                    real, imag = lane_lookup(real, mirror), lane_lookup(imag, mirror)
                values.append((real * c - imag * s, real * s + imag * c))
            for residue, (real, imag) in enumerate(small_dft(values)):
                work[side, residue, pl.ds(base, 8), pl.ds(lane, 128)] = real
                work[side, residue, pl.ds(base + TILE, 8), pl.ds(lane, 128)] = imag


def y_finish(extent, work, table_head, table_rest, h_head, h_rest):
    panels = extent // TILE
    per_tile = TILE // panels
    share = 8 // per_tile
    together = 16 // per_tile
    unroll = math.gcd(panels // together, 4)

    @pl.loop(0, panels // together // unroll)
    def _(major):
        for minor in range(unroll):
            step = major * unroll + minor
            products = []
            for i in range(together):
                residue = together * step + i
                low, high = work[0, residue], work[1, residue]
                turned = jnp.concatenate([high[TILE:] - low[TILE:], low[:TILE] - high[:TILE]], axis=0)
                head, rest = halves(jnp.concatenate([low + high, turned], axis=1))
                products.append(dot_exact(table_head[residue], table_rest[residue], head, rest))
            for part in range(2):
                rows = slice(part * TILE, (part + 1) * TILE)
                grouped = [product[rows].reshape(TILE // 8, 8, -1) for product in products]
                at = pl.multiple_of(part * TILE + step * 16, 16)
                for place in range(share):
                    cut = slice(place * per_tile, (place + 1) * per_tile)
                    head, rest = halves(jnp.concatenate([group[:, cut] for group in grouped], axis=1))
                    h_head[:, place, pl.ds(at, 16), :] = head
                    h_rest[:, place, pl.ds(at, 16), :] = rest


def build_taps(taps_ref):
    support, over = taps_ref.shape
    lane = lax.broadcasted_iota(jnp.int32, (1, over * support), 1)
    table = jnp.zeros((1, over * support), jnp.float32)
    for o in range(over):
        for k in range(support):
            table = jnp.where(lane == k * over + (over - 1 - o), taps_ref[k, o], table)
    return table


def plane_kernel(
    extent, unroll,
    planes_ref, tiles_ref, w_ref, kernel_ref, pos_ref, sky_hbm, basis_ref, y_head, y_rest, e_both,
    out_ref,
    sky, phases, work, h_head, h_rest, yh, yr, eb, turns, rows_head, rows_rest, tile_head, tile_rest,
    send, asked, asked_tiles, values, answers, taps,
    local_sems, request_send, request_recv, answer_send, answer_recv, tile_sems,
):
    tiles_across = extent // TILE
    columns = sky.shape[2]
    lanes = columns // 2
    share = h_head.shape[1]
    planes, slabs = lax.axis_size("ba"), lax.axis_size("wa")
    devices = planes * slabs
    plane, slab = lax.axis_index("ba"), lax.axis_index("wa")
    me = plane * slabs + slab
    blocks, _, samples = pos_ref.shape
    capacity = send.shape[1]
    support, over = kernel_ref.shape
    per = TILE // tiles_across

    loads = [
        pltpu.make_async_copy(
            sky_hbm.at[:, :, pl.ds(i * lanes, lanes)], sky.at[:, :, pl.ds(i * lanes, lanes)], local_sems.at[i]
        )
        for i in range(2)
    ]
    copies = [
        pltpu.make_async_copy(source, target, local_sems.at[2 + i])
        for i, (source, target) in enumerate(((y_head, yh), (y_rest, yr), (e_both, eb)))
    ]
    for copy in loads + copies:
        copy.start()

    def peer(offset):
        index = lax.rem(me + offset, devices)
        return index, {"ba": index // slabs, "wa": index % slabs}

    barrier = pltpu.get_barrier_semaphore()

    @pl.loop(1, devices)
    def _(offset):
        pl.semaphore_signal(
            barrier, inc=1, device_id=peer(offset)[1], device_id_type=pl.DeviceIdType.MESH
        )

    @pl.loop(0, planes)
    def _(p):
        count = jnp.int32(0)
        found = [jnp.int32(0)] * capacity
        for b in range(blocks):
            match = planes_ref[0, b] == p
            for c in range(capacity):
                found[c] = jnp.where(match & (count == c), b, found[c])
            count = count + jnp.where(match, 1, 0)
        for c in range(capacity):
            b = found[c]
            for axis in range(2):
                send[p, c : c + 1, axis * samples : (axis + 1) * samples] = pos_ref[b, axis : axis + 1, :]
            send[p, c : c + 1, 2 * samples :] = jnp.full((1, 128), tiles_ref[b], jnp.int32)

    taps[...] = build_taps(kernel_ref)
    cell = lax.broadcasted_iota(jnp.int32, (tiles_across, TILE), 0) * TILE
    cell = cell + lax.broadcasted_iota(jnp.int32, (tiles_across, TILE), 1)
    angle = (cell * (2 * columns * slab + columns - 1)) % (2 * extent)
    angle = angle.astype(jnp.float32) * (-math.pi / extent)
    turns[0] = jnp.cos(angle) * (1.0 / extent)
    turns[1] = jnp.sin(angle) * (1.0 / extent)

    def request(offset):
        index, where = peer(offset)
        return pltpu.make_async_remote_copy(
            src_ref=send.at[index // slabs],
            dst_ref=asked.at[me],
            send_sem=request_send.at[offset],
            recv_sem=request_recv.at[offset],
            device_id=where,
            device_id_type=pl.DeviceIdType.MESH,
        )

    def tile_copy(offset):
        owner = peer(offset)[0]
        return pltpu.make_async_copy(
            asked.at[owner, :, pl.ds(2 * samples, 128)], asked_tiles.at[owner], tile_sems.at[offset - 1]
        )

    def receive(first):
        for o in range(unroll):
            offset = first + o

            @pl.when(offset < devices)
            def _():
                request(devices - offset).wait_recv()

            tile_copy(offset).start()

    first = slab * columns + lanes
    y_phases(extent, first - 1, -1, lanes, w_ref[0], basis_ref, phases)
    loads[0].wait()
    y_combine(extent, 0, lanes, sky, phases, work)
    pl.semaphore_wait(barrier, devices - 1)

    @pl.loop(1, devices)
    def _(i):
        request(devices - i).start()

    asked[me] = send[plane]
    rows_head[...] = jnp.zeros_like(rows_head)
    rows_rest[...] = jnp.zeros_like(rows_rest)
    tile_head[...] = jnp.zeros_like(tile_head)
    tile_rest[...] = jnp.zeros_like(tile_rest)
    y_phases(extent, first, 1, lanes, w_ref[0], basis_ref, phases)
    loads[1].wait()
    y_combine(extent, 1, lanes, sky, phases, work)
    copies[0].wait()
    copies[1].wait()
    receive(1)
    y_finish(extent, work, yh, yr, h_head, h_rest)
    copies[2].wait()

    row = lax.broadcasted_iota(jnp.int32, (8, 128), 0)
    table = jnp.broadcast_to(taps[...], (8, 128))

    def look_up(tap, position):
        return lane_lookup(table, ((tap * over) | ((over - 1) - (position & (over - 1)))) & 127)

    def form_tile(tile):
        row_tile = tile // tiles_across
        col_tile = tile % tiles_across
        group, place = col_tile // share, col_tile % share
        table = eb[row_tile]
        both = jnp.dot(
            jnp.concatenate([h_head[group, place], h_rest[group, place]], axis=1),
            jnp.concatenate([table, table], axis=0),
            preferred_element_type=jnp.float32,
        )
        both = both[:, :TILE] + both[:, TILE:]
        real, imag = both[:TILE], both[TILE:]
        turn_real, turn_imag = turns[0, pl.ds(row_tile, 1), :], turns[1, pl.ds(row_tile, 1), :]
        return halves(
            jnp.concatenate(
                [real * turn_real - imag * turn_imag, real * turn_imag + imag * turn_real], axis=0
            )
        )

    def row_weights(spot, owner, place):
        for lane in range(0, samples, 128):
            position = asked[owner, place : place + 1, lane : lane + 128]
            cell = position // over
            inner = cell & 7
            value = look_up((row - inner) & 7, position)
            at = (cell // 8) + jnp.where(row < inner, 1, 0)
            parts = [part.astype(jnp.float32) for part in halves(value)]
            for pair in range(0, TILE // 8, 2):
                hits = [at == pair, at == pair + 1]
                for part, target in zip(parts, (rows_head, rows_rest)):
                    target[spot, pair * 8 : pair * 8 + 16, lane : lane + 128] = jnp.concatenate(
                        [jnp.where(hit, part, 0.0) for hit in hits], axis=0
                    ).astype(target.dtype)

    def predict(spot, owner, place):
        slot = spot % 2
        part = dot_exact(tile_head[slot], tile_rest[slot], rows_head[spot], rows_rest[spot])
        for lane in range(0, samples, 128):
            at = samples + lane
            position = asked[owner, place : place + 1, at : at + 128]
            cell = position // over
            column = []
            for j in range(0, tiles_across, 8):
                tap = (row + j - cell) & (tiles_across - 1)
                column.append(jnp.where(tap < support, look_up(tap, position), 0.0))
            away = row * tiles_across - cell
            sums = [jnp.zeros((8, 128), jnp.float32)] * 2
            for j in range(tiles_across):
                hit = ((away + j) & -tiles_across) == 0
                weight = jnp.where(hit, column[j // 8][j % 8 : j % 8 + 1], 0.0)
                for c in range(2):
                    cut = c * TILE + j * per
                    sums[c] = sums[c] + part[cut : cut + per, lane : lane + 128] * weight
            for c in range(2):
                at = c * samples + lane
                values[owner, place : place + 1, at : at + 128] = jnp.sum(sums[c], axis=0, keepdims=True)

    def answer(offset):
        index, where = peer(offset)
        return pltpu.make_async_remote_copy(
            src_ref=values.at[index],
            dst_ref=answers.at[me],
            send_sem=answer_send.at[offset],
            recv_sem=answer_recv.at[offset],
            device_id=where,
            device_id_type=pl.DeviceIdType.MESH,
        )

    steps = devices // unroll
    work_list = [(o + 1, c) for o in range(unroll) for c in range(capacity)]

    @pl.loop(0, steps)
    def _(step):
        begin = step * unroll

        @pl.when(step < steps - 1)
        def _():
            receive(begin + unroll + 1)

        for o in range(unroll):
            tile_copy(begin + o + 1).wait()

        owners = [peer(begin + o)[0] for o in range(unroll + 1)]
        tiles = [asked_tiles[owners[o], c, 0] for o, c in work_list]
        last = len(work_list) - 1
        for spot, (o, c) in enumerate(work_list):
            row_weights(spot, owners[o], c)
            pair = form_tile(tiles[spot])
            if spot:
                predict(spot - 1, owners[work_list[spot - 1][0]], work_list[spot - 1][1])
            else:
                predict(last, owners[0], capacity - 1)
            tile_head[spot % 2], tile_rest[spot % 2] = pair

        @pl.when(step > 0)
        def _():
            answer(begin).start()

        for o in range(1, unroll):
            answer(begin + o).start()

    predict(len(work_list) - 1, me, capacity - 1)
    answers[me] = values[me]

    @pl.loop(1, devices)
    def _(offset):
        request(offset).wait_send()
        answer(offset).wait()

    @pl.loop(0, blocks)
    def _(b):
        p = planes_ref[0, b]
        k = jnp.int32(0)
        for earlier in range(blocks):
            k = k + jnp.where((planes_ref[0, earlier] == p) & (earlier < b), 1, 0)
        total = answers[p * slabs]
        for a in range(1, slabs):
            total += answers[p * slabs + a]
        own = total[0:1]
        for place in range(1, capacity):
            own = jnp.where(k == place, total[place : place + 1], own)
        for c in range(2):
            out_ref[b, c : c + 1, :] = own[:, c * samples : (c + 1) * samples]


def shards(sky_model, plane_w, kernel, tile_ids, plane_ids, positions, observed):
    extent, columns = sky_model.shape[1:]
    planes, slabs = lax.axis_size("ba"), lax.axis_size("wa")
    devices = planes * slabs
    block_count, _, samples = positions.shape
    tiles_across = extent // TILE
    capacity = max(2, block_count // planes)
    smem = pl.BlockSpec(memory_space=pltpu.SMEM)
    vmem = pl.BlockSpec(memory_space=pltpu.VMEM)
    hbm = pl.BlockSpec(memory_space=pl.ANY)
    length = 2 * samples + 128

    lanes = columns // 2
    share = tiles_across * 8 // TILE
    unroll = math.gcd(devices, 4)
    over, support = kernel.shape
    y_head, y_rest = y_tables(extent)
    e_both = x_tables(extent, columns)
    basis = jnp.asarray(interpolation(16))
    half = jnp.bfloat16
    dma = pltpu.SemaphoreType.DMA
    predicted = pl.pallas_call(
        functools.partial(plane_kernel, extent, unroll),
        in_specs=[smem, smem, smem, smem, vmem, hbm, vmem, hbm, hbm, hbm],
        out_specs=vmem,
        out_shape=jax.ShapeDtypeStruct(observed.shape, jnp.float32),
        scratch_shapes=[
            pltpu.VMEM((2, extent, columns), jnp.float32),
            pltpu.VMEM((tiles_across, TILE, 2 * lanes), jnp.float32),
            pltpu.VMEM((2, tiles_across, 2 * TILE, lanes), jnp.float32),
            pltpu.VMEM((tiles_across // share, share, 2 * TILE, columns), half),
            pltpu.VMEM((tiles_across // share, share, 2 * TILE, columns), half),
            pltpu.VMEM(y_head.shape, half),
            pltpu.VMEM(y_head.shape, half),
            pltpu.VMEM(e_both.shape, half),
            pltpu.VMEM((2, tiles_across, TILE), jnp.float32),
            pltpu.VMEM((unroll * capacity, TILE, samples), half),
            pltpu.VMEM((unroll * capacity, TILE, samples), half),
            pltpu.VMEM((2, 2 * TILE, TILE), half),
            pltpu.VMEM((2, 2 * TILE, TILE), half),
            pltpu.VMEM((planes, capacity, length), jnp.int32),
            pltpu.VMEM((devices, capacity, length), jnp.int32),
            pltpu.SMEM((devices, capacity, 128), jnp.int32),
            pltpu.VMEM((devices, capacity, 2 * samples), jnp.float32),
            pltpu.VMEM((devices, capacity, 2 * samples), jnp.float32),
            pltpu.VMEM((1, over * support), jnp.float32),
            dma((5,)),
            dma((devices,)),
            dma((devices,)),
            dma((devices,)),
            dma((devices,)),
            dma((devices,)),
        ],
        compiler_params=pltpu.CompilerParams(
            vmem_limit_bytes=60 << 20, collective_id=0, has_side_effects=True
        ),
        name="plane",
    )(
        plane_ids.T, tile_ids, plane_w, kernel.T, positions, sky_model, basis,
        jnp.asarray(y_head), jnp.asarray(y_rest), jnp.asarray(e_both),
    )
    return observed - predicted


def solution(mesh):
    return jax.shard_map(
        shards,
        mesh=mesh,
        in_specs=(
            P(None, None, "wa"),
            P("ba"),
            P(),
            P(("ba", "wa")),
            P(("ba", "wa"), None),
            P(("ba", "wa"), None, None),
            P(("ba", "wa"), None, None),
        ),
        out_specs=P(("ba", "wa"), None, None),
        check_vma=False,
    )
```

time: 63.2 us -> 47.4 us (0.75)
  Pallas kernels: 58.1 us -> 45 us
  local copies, waits for them, and re-layouts: 2.69 us -> 0.01 us
    pallas_call x1, Pallas kernels: 58.1 us -> 45 us  [shards(): pl.pallas_call(functools.partial(plane_kernel, extent, unroll), in_specs=...]
    unnamed x4 -> x2, local copies, waits for them, and re-layouts: 2.69 us -> 0.01 us
where the time goes in v2:
time: 47.4 us; the launch traced here: 47.2 us
  Pallas kernels  45 us (95%)
  other arithmetic  1.51 us (3%)
  between operations  0.68 us (1%)
    pallas_call x1, Pallas kernels, shards(): pl.pallas_call(functools.partial(plane_kernel, extent, unroll), in_specs=...  45 us
    sub x1, other arithmetic, shards(): return observed - predicted  1.51 us

profile of v2, /device:TPU:0, one launch (start us, length us, event | category | flops | bytes accessed | tf_op | source)
XLA Modules:
  0.0 47.2 jit_solution(12876805428201676388)
XLA Ops:
  0.7 0.0 copy-start
  0.7 45.0 %plane.1 = f32[16,2,512]{2,1,0:T(2,128)} custom-call(s32[1,16]{1,0:T(1,128)} %bitcast.3, s32[16]{0:T(128)} %tiles_ref.1, f32[1]{0:T(128)S(6)} %copy.12.w_ref, f32[8,16]{1,0:T(8,128)} %bitcast.2, s32[16,2,512]{2,1,0:T(2,128)} %pos_ref.1, f32[2,2048,512]{2,1,0:T(8,128)} %sky_hbm.1, bf16[128,48]{1,0:T(8,128)(2,1)} %constant.8.clone.basis_ref, ...), custom_call_target="tpu_custom_call" | custom-call | tf_op jit(solution)/shard_map/plane/pallas_call | solution.py:493
  45.6 0.0 copy-done
  45.7 1.5 %sub.3 = f32[16,2,512]{2,1,0:T(2,128)} subtract(f32[16,2,512]{2,1,0:T(2,128)S(1)} %copy-done, f32[16,2,512]{2,1,0:T(2,128)} %plane.1) | non-fusion elementwise | flops 16384 | bytes 196608 | tf_op jit(solution)/shard_map/sub | solution.py:533
Async XLA Ops:
  0.7 45.0 %copy-start = (f32[16,2,512]{2,1,0:T(2,128)S(1)}, f32[16,2,512]{2,1,0:T(2,128)}, u32[]{:S(2)}) copy-start(f32[16,2,512]{2,1,0:T(2,128)} %param.17) | copy-start | bytes 196612

commit v3 on v2

--- a/solution.py
+++ b/solution.py
@@ -67,7 +67,7 @@
 def small_dft(values):
     count = len(values)
     if count == 1:
-        return values
+        return [values[0]()]
     even = small_dft(values[0::2])
     odd = small_dft(values[1::2])
     low, high = [], []
@@ -158,14 +158,14 @@
 def y_combine(extent, side, lanes, sky_ref, phases, work):
     panels = extent // TILE
 
-    @pl.loop(0, TILE // 8)
+    @pl.loop(0, TILE // 8, unroll=4)
     def _(group):
         base = pl.multiple_of(group * 8, 8)
         mirror = 127 - lax.broadcasted_iota(jnp.int32, (8, 128), 1)
         for lane in range(0, lanes, 128):
             at = lanes + lane if side else lanes - 128 - lane
-            values = []
-            for panel in range(panels):
+
+            def value(panel):
                 c = phases[panel, pl.ds(base, 8), pl.ds(lane, 128)]
                 s = phases[panel, pl.ds(base, 8), pl.ds(lanes + lane, 128)]
                 real, imag = (
@@ -173,7 +173,9 @@
                 )
                 if not side:
                     real, imag = lane_lookup(real, mirror), lane_lookup(imag, mirror)
-                values.append((real * c - imag * s, real * s + imag * c))
+                return real * c - imag * s, real * s + imag * c
+
+            values = [functools.partial(value, panel) for panel in range(panels)]
             for residue, (real, imag) in enumerate(small_dft(values)):
                 work[side, residue, pl.ds(base, 8), pl.ds(lane, 128)] = real
                 work[side, residue, pl.ds(base + TILE, 8), pl.ds(lane, 128)] = imag
@@ -220,8 +222,9 @@
 
 def plane_kernel(
     extent, unroll,
-    planes_ref, tiles_ref, w_ref, kernel_ref, pos_ref, sky_hbm, basis_ref, y_head, y_rest, e_both,
+    planes_hbm, tiles_hbm, w_ref, kernel_hbm, pos_hbm, sky_hbm, basis_hbm, y_head, y_rest, e_both,
     out_ref,
+    planes_ref, tiles_ref, kernel_ref, pos_ref, basis_ref,
     sky, phases, work, h_head, h_rest, yh, yr, eb, turns, rows_head, rows_rest, tile_head, tile_rest,
     send, asked, asked_tiles, values, answers, taps,
     local_sems, request_send, request_recv, answer_send, answer_recv, tile_sems,
@@ -249,7 +252,16 @@
         pltpu.make_async_copy(source, target, local_sems.at[2 + i])
         for i, (source, target) in enumerate(((y_head, yh), (y_rest, yr), (e_both, eb)))
     ]
-    for copy in loads + copies:
+    small = [
+        pltpu.make_async_copy(source, target, local_sems.at[5 + i])
+        for i, (source, target) in enumerate(
+            (
+                (basis_hbm, basis_ref), (planes_hbm, planes_ref), (tiles_hbm, tiles_ref),
+                (kernel_hbm, kernel_ref), (pos_hbm, pos_ref),
+            )
+        )
+    ]
+    for copy in small + loads + copies:
         copy.start()
 
     def peer(offset):
@@ -263,6 +275,12 @@
         pl.semaphore_signal(
             barrier, inc=1, device_id=peer(offset)[1], device_id_type=pl.DeviceIdType.MESH
         )
+
+    first = slab * columns + lanes
+    small[0].wait()
+    y_phases(extent, first - 1, -1, lanes, w_ref[0], basis_ref, phases)
+    for copy in small[1:]:
+        copy.wait()
 
     @pl.loop(0, planes)
     def _(p):
@@ -314,8 +332,6 @@
 
             tile_copy(offset).start()
 
-    first = slab * columns + lanes
-    y_phases(extent, first - 1, -1, lanes, w_ref[0], basis_ref, phases)
     loads[0].wait()
     y_combine(extent, 0, lanes, sky, phases, work)
     pl.semaphore_wait(barrier, devices - 1)
@@ -325,10 +341,11 @@
         request(devices - i).start()
 
     asked[me] = send[plane]
-    rows_head[...] = jnp.zeros_like(rows_head)
-    rows_rest[...] = jnp.zeros_like(rows_rest)
-    tile_head[...] = jnp.zeros_like(tile_head)
-    tile_rest[...] = jnp.zeros_like(tile_rest)
+    last = rows_head.shape[0] - 1
+    rows_head[last] = jnp.zeros(rows_head.shape[1:], rows_head.dtype)
+    rows_rest[last] = jnp.zeros(rows_rest.shape[1:], rows_rest.dtype)
+    tile_head[1] = jnp.zeros(tile_head.shape[1:], tile_head.dtype)
+    tile_rest[1] = jnp.zeros(tile_rest.shape[1:], tile_rest.dtype)
     y_phases(extent, first, 1, lanes, w_ref[0], basis_ref, phases)
     loads[1].wait()
     y_combine(extent, 1, lanes, sky, phases, work)
@@ -478,7 +495,7 @@
     capacity = max(2, block_count // planes)
     smem = pl.BlockSpec(memory_space=pltpu.SMEM)
     vmem = pl.BlockSpec(memory_space=pltpu.VMEM)
-    hbm = pl.BlockSpec(memory_space=pl.ANY)
+    hbm = pl.BlockSpec(memory_space=pltpu.HBM)
     length = 2 * samples + 128
 
     lanes = columns // 2
@@ -492,10 +509,15 @@
     dma = pltpu.SemaphoreType.DMA
     predicted = pl.pallas_call(
         functools.partial(plane_kernel, extent, unroll),
-        in_specs=[smem, smem, smem, smem, vmem, hbm, vmem, hbm, hbm, hbm],
+        in_specs=[hbm, hbm, smem, hbm, hbm, hbm, hbm, hbm, hbm, hbm],
         out_specs=vmem,
-        out_shape=jax.ShapeDtypeStruct(observed.shape, jnp.float32),
+        out_shape=pltpu.VMEM(observed.shape, jnp.float32),
         scratch_shapes=[
+            pltpu.SMEM((1, block_count), jnp.int32),
+            pltpu.SMEM((block_count,), jnp.int32),
+            pltpu.SMEM((support, over), jnp.float32),
+            pltpu.VMEM(positions.shape, jnp.int32),
+            pltpu.VMEM(basis.shape, half),
             pltpu.VMEM((2, extent, columns), jnp.float32),
             pltpu.VMEM((tiles_across, TILE, 2 * lanes), jnp.float32),
             pltpu.VMEM((2, tiles_across, 2 * TILE, lanes), jnp.float32),
@@ -515,7 +537,7 @@
             pltpu.VMEM((devices, capacity, 2 * samples), jnp.float32),
             pltpu.VMEM((devices, capacity, 2 * samples), jnp.float32),
             pltpu.VMEM((1, over * support), jnp.float32),
-            dma((5,)),
+            dma((10,)),
             dma((devices,)),
             dma((devices,)),
             dma((devices,)),
@@ -523,7 +545,7 @@
             dma((devices,)),
         ],
         compiler_params=pltpu.CompilerParams(
-            vmem_limit_bytes=60 << 20, collective_id=0, has_side_effects=True
+            vmem_limit_bytes=62 << 20, collective_id=0, has_side_effects=True
         ),
         name="plane",
     )(

time: 47.4 us -> 43.6 us (0.920)
  Pallas kernels: 45 us -> 42.1 us
  other arithmetic: 1.51 us -> 0.67 us
    pallas_call x1, Pallas kernels: 45 us -> 42.1 us  [shards(): pl.pallas_call(functools.partial(plane_kernel, extent, unroll), in_specs=...]
    sub x1, other arithmetic: 1.51 us -> 0.67 us  [shards(): return observed - predicted]
where the time goes in v3:
time: 43.6 us; the launch traced here: 43.4 us
  Pallas kernels  42.1 us (97%)
  between operations  0.68 us (2%)
  other arithmetic  0.67 us (2%)
    pallas_call x1, Pallas kernels, shards(): pl.pallas_call(functools.partial(plane_kernel, extent, unroll), in_specs=...  42.1 us

profile of v3, /device:TPU:0, one launch (start us, length us, event | category | flops | bytes accessed | tf_op | source)
XLA Modules:
  0.0 43.4 jit_solution(17960889306638431843)
XLA Ops:
  0.7 0.0 copy-start
  0.7 42.1 %plane.1 = f32[16,2,512]{2,1,0:T(2,128)S(1)} custom-call(s32[1,16]{1,0:T(1,128)} %bitcast.3, s32[16]{0:T(128)} %tiles_hbm.1, f32[1]{0:T(128)S(6)} %copy.12.w_ref, f32[8,16]{1,0:T(8,128)} %bitcast.2, s32[16,2,512]{2,1,0:T(2,128)} %pos_hbm.1, f32[2,2048,512]{2,1,0:T(8,128)} %sky_hbm.1, bf16[128,48]{1,0:T(8,128)(2,1)} %constant.8.clone.basis_hbm, ...), custom_call_target="tpu_custom_call" | custom-call | tf_op jit(solution)/shard_map/plane/pallas_call | solution.py:510
  42.7 0.0 copy-done
  42.7 0.7 %sub.3 = f32[16,2,512]{2,1,0:T(2,128)} subtract(f32[16,2,512]{2,1,0:T(2,128)S(1)} %copy-done, f32[16,2,512]{2,1,0:T(2,128)S(1)} %plane.1) | non-fusion elementwise | flops 16384 | bytes 196608 | tf_op jit(solution)/shard_map/sub | solution.py:555
Async XLA Ops:
  0.7 42.1 %copy-start = (f32[16,2,512]{2,1,0:T(2,128)S(1)}, f32[16,2,512]{2,1,0:T(2,128)}, u32[]{:S(2)}) copy-start(f32[16,2,512]{2,1,0:T(2,128)} %param.17) | copy-start | bytes 196612
